TPU v7x, 32 devices: a whole 2x2x4 slice. The times are simulated.
32 devices in a mesh: inner: 4 (over z), outer: 8 (over y, x, core).
Axes of the slice: x: 2, y: 2, z: 4, core: 2. Of those that a mesh axis runs over, the one named last changes fastest.
Arguments:
- inner_state: float32 [2, 16, 2048], P(None, 'inner', 'outer'), may hold values from -6 to 6
- outer_state: float32 [2, 640, 4096], P(None, 'inner', 'outer'), may hold values from -6 to 6
- energies: float32 [16, 2048], P('inner', 'outer'), may hold values from -2 to 2
- dipole: float32 [16, 2048, 2048], P('inner', 'outer'), may hold values from -0.125 to 0.125
- surface: float32 [16, 40, 2048], P('inner', None, 'outer'), may hold values from -0.125 to 0.125
- thresholds: float32 [640], P('inner'), may hold values from 0 to 2
- coupling_coef: float32 [16, 40, 40], P('inner'), may hold values from -1 to 1
- coupling_pattern: int32 [16, 40, 40], P('inner'), may hold values 0 or 1
- block_sizes: int32 [16], P('inner'), may hold values from 1 to 2048, 30720 in all
- field_strength: float32 [2], replicated, may hold values from 0.5 to 2
Outputs:
- inner_final: float32 [2, 16, 2048], P(None, 'inner', 'outer')
- outer_final: float32 [2, 640, 4096], P(None, 'inner', 'outer')
All inputs are finite; a program needn't handle non-finite values. No bound on the sum of `coupling_pattern` or of `block_sizes` on one device may be relied on, other than what follows from the above.
Results may differ from a plain program's by a relative error of at most 0.0001.
Values sent between devices are 32-bit elements; how exact they have to be, the bound alone decides.
A program may use at most 128 MiB of HBM per device.

v0:
```python
import jax
import jax.numpy as jnp
from jax import lax
from jax.sharding import PartitionSpec as P

STEPS = 2
ORDER = 4
kinetic_scale = 3.125
time_step = 0.1


def from_behind(block, axis, distance):
    devices = range(lax.axis_size(axis))
    route = [(i - distance, i) for i in devices if i - distance in devices]
    return lax.ppermute(block, axis, route)


def spread(shard, axis, root):
    mine = lax.axis_index(axis) == root
    return lax.psum(jnp.where(mine, shard, jnp.zeros_like(shard)), axis)


def with_halo(cells, sides, width):
    for axis, dim in sides:
        count = lax.axis_size(axis)
        ends = count - 1
        head = lax.slice_in_dim(cells, 0, width, axis=dim)
        tail = lax.slice_in_dim(cells, cells.shape[dim] - width, cells.shape[dim], axis=dim)
        cells = jnp.concatenate(
            [
                lax.ppermute(tail, axis, [(i, (i + 1) % count) for i in range(ends)]),
                cells,
                lax.ppermute(head, axis, [((i + 1) % count, i) for i in range(ends)]),
            ],
            axis=dim,
        )
    return cells


def reduce_partials(partial_terms, partial_boundary):
    own_terms = lax.psum_scatter(partial_terms, "outer", scatter_dimension=2, tiled=True)
    boundary = lax.psum(partial_boundary, "outer")
    return (own_terms, boundary)


def local(
    inner_state,
    outer_state,
    energies,
    dipole,
    surface,
    thresholds,
    coupling_coef,
    coupling_pattern,
    block_sizes,
    field_strength,
):
    highest = lax.Precision.HIGHEST
    blocks = dipole.shape[0]
    row_count = dipole.shape[1]
    channels = coupling_coef.shape[1]
    radial = outer_state.shape[2]
    sector_index = lax.axis_index("outer")
    row_index = sector_index * row_count + jnp.arange(row_count, dtype=jnp.int32)
    live_rows = (row_index[None, :] < block_sizes[:, None]).astype(jnp.float32)
    coupling = coupling_coef * coupling_pattern.astype(jnp.float32)
    first_sector = jnp.where(sector_index == 0, 1.0, 0.0).astype(jnp.float32)
    edge_mask = first_sector * (jnp.arange(radial, dtype=jnp.int32) == 0).astype(jnp.float32)
    prev_dipole, prev_coupling = from_behind((dipole[blocks - 1], coupling[blocks - 1]), "inner", 1)
    current = (inner_state * live_rows, outer_state)
    for time_index in range(STEPS):
        strength = field_strength[time_index]
        taylor_term = current
        accumulated = current
        for power in range(1, ORDER + 1):
            inner_part = taylor_term[0]
            outer_part = taylor_term[1]
            channel_grid = outer_part.reshape(2, blocks, channels, radial)
            next_first, next_channels = from_behind(
                (inner_part[:, 0], channel_grid[:, 0]), "inner", -1
            )
            extended = jnp.concatenate([inner_part, next_first[:, None]], axis=1)
            gathered = lax.all_gather(extended, "outer", axis=2, tiled=True)
            edge_values = spread(outer_part[:, :, 0], "outer", 0)
            forward = jnp.einsum("lij,plj->pli", dipole, gathered[:, 1:], precision=highest)
            grid_next = jnp.concatenate([channel_grid[:, 1:], next_channels[:, None]], axis=1)
            upward = jnp.einsum("lab,plbr->plar", coupling, grid_next, precision=highest)
            partial_boundary = jnp.einsum("lcs,pls->plc", surface, inner_part, precision=highest)
            prev_rows, prev_channels = from_behind(
                (inner_part[:, blocks - 1], channel_grid[:, blocks - 1]), "inner", 1
            )
            source_rows = jnp.concatenate([prev_rows[:, None], inner_part[:, : blocks - 1]], axis=1)
            source_blocks = jnp.concatenate([prev_dipole[None], dipole[: blocks - 1]], axis=0)
            partial_terms = jnp.einsum(
                "lji,plj->pli", source_blocks, source_rows, precision=highest
            )
            backward, boundary = reduce_partials(partial_terms, partial_boundary)
            source_grid = jnp.concatenate(
                [prev_channels[:, None], channel_grid[:, : blocks - 1]], axis=1
            )
            source_coupling = jnp.concatenate([prev_coupling[None], coupling[: blocks - 1]], axis=0)
            downward = jnp.einsum("lba,plbr->plar", source_coupling, source_grid, precision=highest)
            first_point = edge_values.reshape(2, blocks, channels)
            surf_term = jnp.einsum("lcs,plc->pls", surface, first_point, precision=highest)
            inner_image = live_rows * (
                energies * inner_part + strength * (forward + backward) - kinetic_scale * surf_term
            )
            padded = with_halo(outer_part, (("outer", 2),), 1)
            left_cells = (
                padded[:, :, :radial]
                + edge_mask[None, None, :] * boundary.reshape(2, blocks * channels)[:, :, None]
            )
            right_cells = padded[:, :, 2:]
            kinetic = kinetic_scale * (2.0 * outer_part - left_cells - right_cells)
            outer_image = (
                kinetic
                + thresholds[None, :, None] * outer_part
                + strength * (upward + downward).reshape(2, blocks * channels, radial)
            )
            inner_image, outer_image = (inner_image, outer_image)
            factor = time_step / power
            taylor_term = (
                factor * jnp.stack([inner_image[1], -inner_image[0]]),
                factor * jnp.stack([outer_image[1], -outer_image[0]]),
            )
            accumulated = (accumulated[0] + taylor_term[0], accumulated[1] + taylor_term[1])
        current = accumulated
    return (current[0], current[1])


def solution(mesh):
    placed = (
        P(None, "inner", "outer"),
        P(None, "inner", "outer"),
        P("inner", "outer"),
        P("inner", "outer", None),
        P("inner", None, "outer"),
        P("inner"),
        P("inner", None, None),
        P("inner", None, None),
        P("inner"),
        P(),
    )
    return jax.shard_map(
        local,
        mesh=mesh,
        in_specs=placed,
        out_specs=(P(None, "inner", "outer"), P(None, "inner", "outer")),
        check_vma=False,
    )
```

profile of v0, /device:TPU:12, one launch (start us, length us, event | category | flops | bytes accessed | tf_op | source)
XLA Modules:
  0.0 834.8 jit_solution(18084127534141652575)
XLA Ops:
  34.9 12.6 %all-reduce.7 = (f32[2,160]{1,0:T(2,128)}, f32[2,4,40]{2,0,1:T(2,128)S(1)}) all-reduce(f32[2,160]{1,0:T(2,128)S(1)} %mul.616, f32[2,4,40]{2,0,1:T(2,128)S(1)} %copy.69), channel_id=1, replica_groups=mesh['inner'=4,'outer'=8] {'outer'}, use_global_device_ids=true, to_apply=%region_3.4 | all-reduce | flops 640 | bytes 5120 | tf_op jit(solution)/shard_map/psum | solution.py:42
  59.9 8.3 all_gather.24
  117.4 30.5 %reduce-scatter.25.cloned.1.call-done = f32[256,8]{1,0:T(8,128)} async-done(((f32[2048,8]{1,0:T(8,128)}), f32[256,8]{1,0:T(8,128)}) %reduce-scatter.25.cloned.1.call-update) | async-done | bytes 8208
  151.2 9.8 %fusion.55 = f32[2,4,256]{2,0,1:T(2,128)S(1)} fusion(f32[2,4,256]{2,0,1:T(2,128)S(1)} %fusion.63, f32[2,4,256]{2,0,1:T(2,128)S(1)} %copy.138, f32[2,5,2048]{2,0,1:T(2,128)S(1)} %all_gather.24, f32[4,256,2048]{2,1,0:T(8,128)} %param.13, f32[2,4,256]{2,0,1:T(2,128)S(1)} %copy-done.49, f32[]{:T(128)} %bitcast, f32[4,256]{1,0:T(4,128)S(1)} %copy-done.53, ...), kind=kOutput, calls=%fused_computation.81 | convolution fusion | flops 50343936 | bytes 8511492 | tf_op jit(solution)/shard_map/lij,plj->pli/dot_general | solution.py:85
  161.4 12.6 %all-reduce.6 = (f32[2,160]{1,0:T(2,128)S(1)}, f32[2,4,40]{2,0,1:T(2,128)S(1)}) all-reduce(f32[2,160]{1,0:T(2,128)S(1)} %mul.639, f32[2,4,40]{2,0,1:T(2,128)S(1)} %copy.79), channel_id=1, replica_groups=mesh['inner'=4,'outer'=8] {'outer'}, use_global_device_ids=true, to_apply=%region_6.7 | all-reduce | flops 640 | bytes 5120 | tf_op jit(solution)/shard_map/psum | solution.py:42
  221.3 28.3 %reduce-scatter.27.cloned.1.call-done = f32[256,8]{1,0:T(8,128)} async-done(((f32[2048,8]{1,0:T(8,128)}), f32[256,8]{1,0:T(8,128)}) %reduce-scatter.27.cloned.1.call-update) | async-done | bytes 8208
  252.8 9.8 %fusion.50 = f32[2,4,256]{2,0,1:T(2,128)S(1)} fusion(f32[2,4,256]{2,0,1:T(2,128)S(1)} %fusion.62, f32[2,4,256]{2,0,1:T(2,128)S(1)} %copy.140, f32[2,5,2048]{2,0,1:T(2,128)S(1)} %all_gather.25, f32[4,256,2048]{2,1,0:T(8,128)} %param.13, f32[4,256]{1,0:T(4,128)S(1)} %get-tuple-element.129, f32[]{:T(128)} %bitcast, f32[4,256]{1,0:T(4,128)S(1)} %compare_convert_fusion, ...), kind=kOutput, calls=%fused_computation.75 | convolution fusion | flops 50345984 | bytes 8511492 | tf_op jit(solution)/shard_map/lij,plj->pli/dot_general | solution.py:85
  266.4 12.8 %all-reduce.5 = (f32[2,160]{1,0:T(2,128)}, f32[2,4,40]{2,0,1:T(2,128)S(1)}) all-reduce(f32[2,160]{1,0:T(2,128)S(1)} %mul.662, f32[2,4,40]{2,0,1:T(2,128)S(1)} %copy.83), channel_id=1, replica_groups=mesh['inner'=4,'outer'=8] {'outer'}, use_global_device_ids=true, to_apply=%region_9.10 | all-reduce | flops 640 | bytes 5120 | tf_op jit(solution)/shard_map/psum | solution.py:42
  296.6 8.4 %all_gather.26 = f32[2,5,2048]{2,0,1:T(2,128)S(1)} all-gather(f32[2,5,256]{2,0,1:T(2,128)S(1)} %pad_maximum_fusion.25), channel_id=1, replica_groups=mesh['inner'=4,'outer'=8] {'outer'}, dimensions={2}, use_global_device_ids=true | all-gather | bytes 92160 | tf_op jit(solution)/shard_map/all_gather | solution.py:83
  336.2 9.8 %fusion.45 = f32[2,4,256]{2,0,1:T(2,128)S(1)} fusion(f32[2,4,256]{2,0,1:T(2,128)S(1)} %fusion.61, f32[2,4,256]{2,0,1:T(2,128)S(1)} %copy.142, f32[2,5,2048]{2,0,1:T(2,128)S(1)} %all_gather.26, f32[4,256,2048]{2,1,0:T(8,128)} %param.13, f32[4,256]{1,0:T(4,128)S(1)} %get-tuple-element.130, f32[]{:T(128)} %bitcast, f32[4,256]{1,0:T(4,128)S(1)} %compare_convert_fusion, ...), kind=kOutput, calls=%fused_computation.69 | convolution fusion | flops 50345984 | bytes 8511492 | tf_op jit(solution)/shard_map/lij,plj->pli/dot_general | solution.py:85
  350.1 12.7 %all-reduce.4 = (f32[2,160]{1,0:T(2,128)}, f32[2,4,40]{2,0,1:T(2,128)S(1)}) all-reduce(f32[2,160]{1,0:T(2,128)S(1)} %mul.684, f32[2,4,40]{2,0,1:T(2,128)} %copy.87), channel_id=1, replica_groups=mesh['inner'=4,'outer'=8] {'outer'}, use_global_device_ids=true, to_apply=%region_12.13 | all-reduce | flops 640 | bytes 5120 | tf_op jit(solution)/shard_map/psum | solution.py:42
  388.6 28.1 %reduce-scatter.31.cloned.1.call-done = f32[256,8]{1,0:T(8,128)} async-done(((f32[2048,8]{1,0:T(8,128)}), f32[256,8]{1,0:T(8,128)}) %reduce-scatter.31.cloned.1.call-update) | async-done | bytes 8208
  419.8 9.8 %fusion.40 = f32[2,4,256]{2,0,1:T(2,128)S(1)} fusion(f32[2,4,256]{2,0,1:T(2,128)} %fusion.60, f32[2,4,256]{2,0,1:T(2,128)S(1)} %copy.144, f32[2,5,2048]{2,0,1:T(2,128)S(1)} %all_gather.27, f32[4,256,2048]{2,1,0:T(8,128)} %param.13, f32[4,256]{1,0:T(4,128)S(1)} %get-tuple-element.128, f32[]{:T(128)} %bitcast, f32[4,256]{1,0:T(4,128)S(1)} %compare_convert_fusion, ...), kind=kOutput, calls=%fused_computation.63 | convolution fusion | flops 50345984 | bytes 8511492 | tf_op jit(solution)/shard_map/lij,plj->pli/dot_general | solution.py:85
  453.2 8.3 all_gather.28
  472.7 14.2 %all-reduce.3 = (f32[2,160]{1,0:T(2,128)}, f32[2,4,40]{2,0,1:T(2,128)}) all-reduce(f32[2,160]{1,0:T(2,128)} %mul.704, f32[2,4,40]{2,0,1:T(2,128)S(1)} %copy.91), channel_id=1, replica_groups=mesh['inner'=4,'outer'=8] {'outer'}, use_global_device_ids=true, to_apply=%region_15.16 | all-reduce | flops 640 | bytes 5120 | tf_op jit(solution)/shard_map/psum | solution.py:42
  505.6 9.8 %fusion.35 = f32[2,4,256]{2,0,1:T(2,128)S(1)} fusion(f32[2,4,256]{2,0,1:T(2,128)} %fusion.59, f32[2,4,256]{2,0,1:T(2,128)} %copy.146, f32[2,5,2048]{2,0,1:T(2,128)S(1)} %all_gather.28, f32[4,256,2048]{2,1,0:T(8,128)} %param.13, f32[2,4,256]{2,0,1:T(2,128)S(1)} %fusion.196, f32[]{:T(128)} %bitcast.65, f32[4,256]{1,0:T(4,128)S(1)} %copy-done.53, ...), kind=kOutput, calls=%fused_computation.57 | convolution fusion | flops 50343936 | bytes 8511492 | tf_op jit(solution)/shard_map/lij,plj->pli/dot_general | solution.py:85
  557.7 14.5 %all-reduce.2 = (f32[2,160]{1,0:T(2,128)}, f32[2,4,40]{2,0,1:T(2,128)}) all-reduce(f32[2,160]{1,0:T(2,128)} %mul.721, f32[2,4,40]{2,0,1:T(2,128)S(1)} %copy.99), channel_id=1, replica_groups=mesh['inner'=4,'outer'=8] {'outer'}, use_global_device_ids=true, to_apply=%region_18.19 | all-reduce | flops 640 | bytes 5120 | tf_op jit(solution)/shard_map/psum | solution.py:42
  590.5 9.8 %fusion.30 = f32[2,4,256]{2,0,1:T(2,128)S(1)} fusion(f32[2,4,256]{2,0,1:T(2,128)} %fusion.58, f32[2,4,256]{2,0,1:T(2,128)} %copy.148, f32[2,5,2048]{2,0,1:T(2,128)S(1)} %all_gather.29, f32[4,256,2048]{2,1,0:T(8,128)} %param.13, f32[]{:T(128)} %bitcast.65, f32[4,256]{1,0:T(4,128)S(1)} %copy-done.55, f32[4,256]{1,0:T(4,128)S(1)} %compare_convert_fusion, ...), kind=kOutput, calls=%fused_computation.51 | convolution fusion | flops 50345984 | bytes 8511492 | tf_op jit(solution)/shard_map/lij,plj->pli/dot_general | solution.py:85
  631.3 28.7 %reduce-scatter.37.cloned.1.call-done = f32[256,8]{1,0:T(8,128)} async-done(((f32[2048,8]{1,0:T(8,128)}), f32[256,8]{1,0:T(8,128)}) %reduce-scatter.37.cloned.1.call-update) | async-done | bytes 8208
  677.2 13.2 %all-reduce.1 = (f32[2,160]{1,0:T(2,128)}, f32[2,4,40]{2,0,1:T(2,128)}) all-reduce(f32[2,160]{1,0:T(2,128)} %mul.738, f32[2,4,40]{2,0,1:T(2,128)} %copy.103), channel_id=1, replica_groups=mesh['inner'=4,'outer'=8] {'outer'}, use_global_device_ids=true, to_apply=%region_21.22 | all-reduce | flops 640 | bytes 5120 | tf_op jit(solution)/shard_map/psum | solution.py:42
  691.3 9.8 %fusion.25 = f32[2,4,256]{2,0,1:T(2,128)S(1)} fusion(f32[2,4,256]{2,0,1:T(2,128)S(1)} %fusion.57, f32[2,4,256]{2,0,1:T(2,128)} %copy.150, f32[2,5,2048]{2,0,1:T(2,128)S(1)} %all_gather.30, f32[4,256,2048]{2,1,0:T(8,128)} %param.13, f32[]{:T(128)} %bitcast.65, f32[4,256]{1,0:T(4,128)S(1)} %get-tuple-element.130, f32[4,256]{1,0:T(4,128)S(1)} %compare_convert_fusion, ...), kind=kOutput, calls=%fused_computation.45 | convolution fusion | flops 50345984 | bytes 8511492 | tf_op jit(solution)/shard_map/lij,plj->pli/dot_general | solution.py:85
  744.0 28.4 %reduce-scatter.39.cloned.1.call-done = f32[256,8]{1,0:T(8,128)} async-done(((f32[2048,8]{1,0:T(8,128)}), f32[256,8]{1,0:T(8,128)}) %reduce-scatter.39.cloned.1.call-update) | async-done | bytes 8208
  795.6 13.1 %all-reduce = (f32[2,4,40]{2,0,1:T(2,128)S(1)}, f32[2,160]{1,0:T(2,128)S(1)}) all-reduce(f32[2,4,40]{2,0,1:T(2,128)S(1)} %copy.107, f32[2,160]{1,0:T(2,128)S(1)} %mul.753), channel_id=1, replica_groups=mesh['inner'=4,'outer'=8] {'outer'}, use_global_device_ids=true, to_apply=%region_22.23 | all-reduce | flops 640 | bytes 5120 | tf_op jit(solution)/shard_map/psum | solution.py:20
  809.1 10.4 %fusion.20 = f32[2,4,256]{2,0,1:T(2,128)S(1)} fusion(f32[2,4,256]{2,0,1:T(2,128)S(1)} %fusion.56, f32[2,4,256]{2,0,1:T(2,128)S(1)} %copy.152, f32[2,5,2048]{2,0,1:T(2,128)S(1)} %all_gather.31, f32[4,256,2048]{2,1,0:T(8,128)} %param.13, f32[]{:T(128)} %bitcast.65, f32[4,256]{1,0:T(4,128)S(1)} %get-tuple-element.128, f32[4,256]{1,0:T(4,128)S(1)} %compare_convert_fusion, ...), kind=kOutput, calls=%fused_computation.39 | convolution fusion | flops 50345984 | bytes 8511492 | tf_op jit(solution)/shard_map/lij,plj->pli/dot_general | solution.py:85
  (492 shorter events, 463.9 us)
Async XLA Ops:
  7.2 140.7 %reduce-scatter.25.cloned.1.call-start = ((), (), s32[]{:S(2)}) async-start(), calls=%async_computation.8 | async-start | bytes 1179648
  8.7 88.7 %collective-permute-start.1 = (f32[2,256]{1,0:T(2,128)S(1)}, f32[2,256]{1,0:T(2,128)S(1)}, u32[]{:S(2)}, u32[]{:S(2)}) collective-permute-start(f32[2,256]{1,0:T(2,128)S(1)} %get-tuple-element.127), channel_id=1, source_target_pairs={{0,8},{8,16},{16,24},{1,9},{9,17},{17,25},{2,10},{10,18},{18,26},{... | collective-permute-start | bytes 6152 | tf_op jit(solution)/shard_map/ppermute | solution.py:15
  15.4 82.0 %collective-permute-start.2 = (f32[256,2048]{1,0:T(8,128)}, f32[256,2048]{1,0:T(8,128)S(1)}, u32[]{:S(2)}, u32[]{:S(2)}) collective-permute-start(f32[256,2048]{1,0:T(8,128)} %slice_bitcast_fusion), channel_id=1, source_target_pairs={{0,8},{8,16},{16,24},{1,9},{9,17},{17,25},{2,10},{10,18},{18,26},{... | collective-permute-start | bytes 6291464 | tf_op jit(solution)/shard_map/ppermute | solution.py:15
  88.5 85.4 %collective-permute-start.12 = (f32[2,160,1]{2,1,0:T(8,128)}, f32[2,160,1]{2,1,0:T(8,128)}, u32[]{:S(2)}, u32[]{:S(2)}) collective-permute-start(f32[2,160,1]{2,1,0:T(8,128)} %get-tuple-element.81), channel_id=1, source_target_pairs={{0,1},{1,2},{2,3},{3,4},{4,5},{5,6},{6,7},{8,9},{9,10},{10,11},{11... | collective-permute-start | bytes 3848 | tf_op jit(solution)/shard_map/ppermute | solution.py:31
  91.3 82.6 %collective-permute-start.13 = (f32[2,160,1]{2,1,0:T(8,128)}, f32[2,160,1]{2,1,0:T(8,128)}, u32[]{:S(2)}, u32[]{:S(2)}) collective-permute-start(f32[2,160,1]{2,1,0:T(8,128)} %get-tuple-element.82), channel_id=1, source_target_pairs={{1,0},{2,1},{3,2},{4,3},{5,4},{6,5},{7,6},{9,8},{10,9},{11,10},{12... | collective-permute-start | bytes 3848 | tf_op jit(solution)/shard_map/ppermute | solution.py:33
  113.7 135.9 %reduce-scatter.27.cloned.1.call-start = ((), (), s32[]{:S(2)}) async-start(), calls=%async_computation.9 | async-start | bytes 1179648
  186.0 119.1 %collective-permute-start.21 = (f32[2,40,512]{2,1,0:T(8,128)}, f32[2,40,512]{2,1,0:T(8,128)}, u32[]{:S(2)}, u32[]{:S(2)}) collective-permute-start(f32[2,40,512]{2,1,0:T(8,128)} %get-tuple-element.77), channel_id=1, source_target_pairs={{0,8},{8,16},{16,24},{1,9},{9,17},{17,25},{2,10},{10,18},{18,26},{... | collective-permute-start | bytes 491528 | tf_op jit(solution)/shard_map/ppermute | solution.py:15
  189.4 117.4 %collective-permute-start.20 = (f32[2,40,512]{2,1,0:T(8,128)}, f32[2,40,512]{2,1,0:T(8,128)}, u32[]{:S(2)}, u32[]{:S(2)}) collective-permute-start(f32[2,40,512]{2,1,0:T(8,128)} %get-tuple-element.76), channel_id=1, source_target_pairs={{8,0},{16,8},{24,16},{9,1},{17,9},{25,17},{10,2},{18,10},{26,18},{... | collective-permute-start | bytes 491528 | tf_op jit(solution)/shard_map/ppermute | solution.py:15
  192.5 116.8 %collective-permute-start.18 = (f32[2,160,1]{2,1,0:T(8,128)}, f32[2,160,1]{2,1,0:T(8,128)}, u32[]{:S(2)}, u32[]{:S(2)}) collective-permute-start(f32[2,160,1]{2,1,0:T(8,128)} %get-tuple-element.72), channel_id=1, source_target_pairs={{0,1},{1,2},{2,3},{3,4},{4,5},{5,6},{6,7},{8,9},{9,10},{10,11},{11... | collective-permute-start | bytes 3848 | tf_op jit(solution)/shard_map/ppermute | solution.py:31
  194.4 114.9 %collective-permute-start.19 = (f32[2,160,1]{2,1,0:T(8,128)}, f32[2,160,1]{2,1,0:T(8,128)}, u32[]{:S(2)}, u32[]{:S(2)}) collective-permute-start(f32[2,160,1]{2,1,0:T(8,128)} %get-tuple-element.73), channel_id=1, source_target_pairs={{1,0},{2,1},{3,2},{4,3},{5,4},{6,5},{7,6},{9,8},{10,9},{11,10},{12... | collective-permute-start | bytes 3848 | tf_op jit(solution)/shard_map/ppermute | solution.py:33
  213.5 119.4 %reduce-scatter.29.cloned.1.call-start = ((), (), s32[]{:S(2)}) async-start(), calls=%async_computation.10 | async-start | bytes 1179648
  296.6 120.0 %reduce-scatter.31.cloned.1.call-start = ((), (), s32[]{:S(2)}) async-start(), calls=%async_computation.11 | async-start | bytes 1179648
  315.8 145.7 %collective-permute-start.27 = (f32[2,40,512]{2,1,0:T(8,128)}, f32[2,40,512]{2,1,0:T(8,128)}, u32[]{:S(2)}, u32[]{:S(2)}) collective-permute-start(f32[2,40,512]{2,1,0:T(8,128)} %get-tuple-element.68), channel_id=1, source_target_pairs={{0,8},{8,16},{16,24},{1,9},{9,17},{17,25},{2,10},{10,18},{18,26},{... | collective-permute-start | bytes 491528 | tf_op jit(solution)/shard_map/ppermute | solution.py:15
  319.2 144.1 %collective-permute-start.26 = (f32[2,40,512]{2,1,0:T(8,128)}, f32[2,40,512]{2,1,0:T(8,128)}, u32[]{:S(2)}, u32[]{:S(2)}) collective-permute-start(f32[2,40,512]{2,1,0:T(8,128)} %get-tuple-element.67), channel_id=1, source_target_pairs={{8,0},{16,8},{24,16},{9,1},{17,9},{25,17},{10,2},{18,10},{26,18},{... | collective-permute-start | bytes 491528 | tf_op jit(solution)/shard_map/ppermute | solution.py:15
  322.3 143.5 %collective-permute-start.24 = (f32[2,160,1]{2,1,0:T(8,128)}, f32[2,160,1]{2,1,0:T(8,128)}, u32[]{:S(2)}, u32[]{:S(2)}) collective-permute-start(f32[2,160,1]{2,1,0:T(8,128)} %get-tuple-element.63), channel_id=1, source_target_pairs={{0,1},{1,2},{2,3},{3,4},{4,5},{5,6},{6,7},{8,9},{9,10},{10,11},{11... | collective-permute-start | bytes 3848 | tf_op jit(solution)/shard_map/ppermute | solution.py:31
  324.2 141.6 %collective-permute-start.25 = (f32[2,160,1]{2,1,0:T(8,128)}, f32[2,160,1]{2,1,0:T(8,128)}, u32[]{:S(2)}, u32[]{:S(2)}) collective-permute-start(f32[2,160,1]{2,1,0:T(8,128)} %get-tuple-element.64), channel_id=1, source_target_pairs={{1,0},{2,1},{3,2},{4,3},{5,4},{6,5},{7,6},{9,8},{10,9},{11,10},{12... | collective-permute-start | bytes 3848 | tf_op jit(solution)/shard_map/ppermute | solution.py:33
  380.5 121.3 %reduce-scatter.33.cloned.1.call-start = ((), (), s32[]{:S(2)}) async-start(), calls=%async_computation.12 | async-start | bytes 1179648
  453.1 133.5 %reduce-scatter.35.cloned.1.call-start = ((), (), s32[]{:S(2)}) async-start(), calls=%async_computation.13 | async-start | bytes 1179648
  538.1 122.0 %reduce-scatter.37.cloned.1.call-start = ((), (), s32[]{:S(2)}) async-start(), calls=%async_computation.14 | async-start | bytes 1179648
  573.7 90.2 %collective-permute-start.39 = (f32[2,40,512]{2,1,0:T(8,128)}, f32[2,40,512]{2,1,0:T(8,128)}, u32[]{:S(2)}, u32[]{:S(2)}) collective-permute-start(f32[2,40,512]{2,1,0:T(8,128)} %get-tuple-element.50), channel_id=1, source_target_pairs={{0,8},{8,16},{16,24},{1,9},{9,17},{17,25},{2,10},{10,18},{18,26},{... | collective-permute-start | bytes 491528 | tf_op jit(solution)/shard_map/ppermute | solution.py:15
  577.5 88.1 %collective-permute-start.38 = (f32[2,40,512]{2,1,0:T(8,128)}, f32[2,40,512]{2,1,0:T(8,128)}, u32[]{:S(2)}, u32[]{:S(2)}) collective-permute-start(f32[2,40,512]{2,1,0:T(8,128)} %get-tuple-element.49), channel_id=1, source_target_pairs={{8,0},{16,8},{24,16},{9,1},{17,9},{25,17},{10,2},{18,10},{26,18},{... | collective-permute-start | bytes 491528 | tf_op jit(solution)/shard_map/ppermute | solution.py:15
  580.2 88.0 %collective-permute-start.36 = (f32[2,160,1]{2,1,0:T(8,128)}, f32[2,160,1]{2,1,0:T(8,128)}, u32[]{:S(2)}, u32[]{:S(2)}) collective-permute-start(f32[2,160,1]{2,1,0:T(8,128)} %get-tuple-element.45), channel_id=1, source_target_pairs={{0,1},{1,2},{2,3},{3,4},{4,5},{5,6},{6,7},{8,9},{9,10},{10,11},{11... | collective-permute-start | bytes 3848 | tf_op jit(solution)/shard_map/ppermute | solution.py:31
  582.1 86.0 %collective-permute-start.37 = (f32[2,160,1]{2,1,0:T(8,128)}, f32[2,160,1]{2,1,0:T(8,128)}, u32[]{:S(2)}, u32[]{:S(2)}) collective-permute-start(f32[2,160,1]{2,1,0:T(8,128)} %get-tuple-element.46), channel_id=1, source_target_pairs={{1,0},{2,1},{3,2},{4,3},{5,4},{6,5},{7,6},{9,8},{10,9},{11,10},{12... | collective-permute-start | bytes 3848 | tf_op jit(solution)/shard_map/ppermute | solution.py:33
  622.9 149.5 %reduce-scatter.39.cloned.1.call-start = ((), (), s32[]{:S(2)}) async-start(), calls=%async_computation.15 | async-start | bytes 1179648
  (108 other events, 2695.7 us)
Sparse Core Ops, SparseCore 0:
  113.8 34.1 reduce-scatter.24
  213.6 35.9 reduce-scatter.26
  296.7 36.1 reduce-scatter.28
  380.6 35.9 reduce-scatter.30
  453.3 36.6 reduce-scatter.32
  538.2 36.7 reduce-scatter.34
  623.1 36.9 reduce-scatter.36
  736.0 36.3 reduce-scatter.38
where the time goes:
time: 847 us; the launch traced here: 835 us
  matrix products  174 us (21%)
  blocking collectives  169 us (20%)
  starting transfers between devices  156 us (18%)
  waiting for transfers between devices  152 us (18%)
  local copies, waits for them, and re-layouts  136 us (16%)
  other arithmetic  31.5 us (4%)
  between operations  17 us (2%)
    unnamed x16, waiting for transfers between devices  148 us
    ppermute x34, starting transfers between devices, from_behind(): return lax.ppermute(block, axis, route)  103 us
    unnamed x181, local copies, waits for them, and re-layouts  95.9 us
    psum x7, blocking collectives, reduce_partials(): boundary = lax.psum(partial_boundary, 'outer')  92.6 us
    dot_general x8, matrix products, local(): jnp.einsum('lij,plj->pli', dipole, gathered[:, 1:], precision=highest)  79.2 us
    all_gather x8, blocking collectives, local(): gathered = lax.all_gather(extended, 'outer', axis=2, tiled=True)  63.2 us
    dot_general x8, matrix products, local(): jnp.einsum('lji,plj->pli', source_blocks, source_rows, precision=highest)  55.2 us
    ppermute x8, starting transfers between devices, with_halo(): lax.ppermute(head, axis, [((i + 1) % count, i) for i in range(ends)])  36.4 us
  transfers between devices with their start and end apart: 58, of which 9 were waited for; matrix products, arithmetic and copies ran while one was open for 36% of the time, Pallas kernels for 0%

commit v1 on v0

--- a/solution.py
+++ b/solution.py
@@ -2,11 +2,25 @@
 import jax.numpy as jnp
 from jax import lax
 from jax.sharding import PartitionSpec as P
+from jax.lax import axis_size, ppermute
 
 STEPS = 2
 ORDER = 4
 kinetic_scale = 3.125
 time_step = 0.1
+
+
+def test_view(body, mesh_name):
+    far_arr, frame_out = (body, 0)
+    slots = axis_size(mesh_name)
+    while 1 << frame_out < slots:
+        vec_out = range(slots)
+        tile_out = map(lambda no: (no, no ^ 1 << frame_out), vec_out)
+        v_next = list(tile_out)
+        found_now = ppermute(far_arr, mesh_name, v_next)
+        far_arr = far_arr + found_now
+        frame_out = frame_out + 1
+    return far_arr
 
 
 def from_behind(block, axis, distance):
@@ -39,7 +53,7 @@
 
 def reduce_partials(partial_terms, partial_boundary):
     own_terms = lax.psum_scatter(partial_terms, "outer", scatter_dimension=2, tiled=True)
-    boundary = lax.psum(partial_boundary, "outer")
+    boundary = test_view(partial_boundary, "outer")
     return (own_terms, boundary)
 
 

time: 847 us -> 864 us (1.020)
  waiting for transfers between devices: 152 us -> 195 us
  blocking collectives: 169 us -> 127 us
    psum x7 -> x0, blocking collectives: 92.6 us -> none  [reduce_partials(): boundary = lax.psum(partial_boundary, 'outer')]
    psum x1 -> x4, blocking collectives: 13.1 us -> 53.1 us  [spread(): return lax.psum(jnp.where(mine, shard, jnp.zeros_like(shard)), axis)]
    unnamed x16, waiting for transfers between devices: 148 us -> 171 us
    ppermute x0 -> x24, waiting for transfers between devices: none -> 15.7 us  [test_view(): found_now = ppermute(far_arr, mesh_name, v_next)]
    all_gather x8, blocking collectives: 63.2 us -> 74.1 us  [local(): gathered = lax.all_gather(extended, 'outer', axis=2, tiled=True)]
    unnamed x181 -> x231, local copies, waits for them, and re-layouts: 95.9 us -> 98.9 us
  transfers between devices with their start and end apart: 58 -> 82, of which waited for: 9 -> 14; matrix products, arithmetic and copies ran while one was open for 36% -> 33% of each run, Pallas kernels for 0% -> 0%
where the time goes in v1:
time: 864 us; the launch traced here: 850 us
  waiting for transfers between devices  195 us (23%)
  matrix products  169 us (20%)
  starting transfers between devices  163 us (19%)
  local copies, waits for them, and re-layouts  140 us (16%)
  blocking collectives  127 us (15%)
  other arithmetic  37.5 us (4%)
  between operations  17.4 us (2%)
    unnamed x16, waiting for transfers between devices  171 us
    ppermute x34, starting transfers between devices, from_behind(): return lax.ppermute(block, axis, route)  105 us
    unnamed x231, local copies, waits for them, and re-layouts  98.9 us
    dot_general x8, matrix products, local(): jnp.einsum('lij,plj->pli', dipole, gathered[:, 1:], precision=highest)  81.3 us
    all_gather x8, blocking collectives, local(): gathered = lax.all_gather(extended, 'outer', axis=2, tiled=True)  74.1 us
    psum x4, blocking collectives, spread(): return lax.psum(jnp.where(mine, shard, jnp.zeros_like(shard)), axis)  53.1 us
    dot_general x8, matrix products, local(): jnp.einsum('lji,plj->pli', source_blocks, source_rows, precision=highest)  47.3 us
    ppermute x8, starting transfers between devices, with_halo(): lax.ppermute(head, axis, [((i + 1) % count, i) for i in range(ends)])  34.3 us
  transfers between devices with their start and end apart: 82, of which 14 were waited for; matrix products, arithmetic and copies ran while one was open for 33% of the time, Pallas kernels for 0%

profile of v1, /device:TPU:12, one launch (start us, length us, event | category | flops | bytes accessed | tf_op | source)
XLA Modules:
  0.0 849.6 jit_solution(8659107928719507220)
XLA Ops:
  48.0 9.8 %all_gather.24 = f32[2,5,2048]{2,0,1:T(2,128)S(1)} all-gather(f32[2,5,256]{2,0,1:T(2,128)S(1)} %pad_maximum_fusion.23), channel_id=1, replica_groups=mesh['inner'=4,'outer'=8] {'outer'}, dimensions={2}, use_global_device_ids=true | all-gather | bytes 92160 | tf_op jit(solution)/shard_map/all_gather | solution.py:97
  80.9 12.1 %all-reduce.3 = (f32[2,4,40]{2,0,1:T(2,128)S(1)}, f32[2,4,40]{2,0,1:T(2,128)S(1)}) all-reduce(f32[2,4,40]{2,0,1:T(2,128)S(1)} %copy.69, f32[2,4,40]{2,0,1:T(2,128)S(1)} %copy.79), channel_id=1, replica_groups=mesh['inner'=4,'outer'=8] {'outer'}, use_global_device_ids=true, to_apply=%region_1.2 | all-reduce | flops 640 | bytes 5120 | tf_op jit(solution)/shard_map/psum | solution.py:34
  135.5 31.8 %reduce-scatter.25.cloned.1.call-done = f32[256,8]{1,0:T(8,128)} async-done(((f32[2048,8]{1,0:T(8,128)}), f32[256,8]{1,0:T(8,128)}) %reduce-scatter.25.cloned.1.call-update) | async-done | bytes 8208
  170.6 10.4 %fusion.55 = f32[2,4,256]{2,0,1:T(2,128)S(1)} fusion(f32[2,4,256]{2,0,1:T(2,128)S(1)} %fusion.63, f32[2,4,256]{2,0,1:T(2,128)S(1)} %copy.138, f32[2,5,2048]{2,0,1:T(2,128)S(1)} %all_gather.24, f32[4,256,2048]{2,1,0:T(8,128)} %param.13, f32[2,4,256]{2,0,1:T(2,128)S(1)} %copy-done.68, f32[]{:T(128)} %bitcast, f32[4,256]{1,0:T(4,128)S(1)} %copy-done.71, ...), kind=kOutput, calls=%fused_computation.81 | convolution fusion | flops 50343936 | bytes 8511492 | tf_op jit(solution)/shard_map/lij,plj->pli/dot_general | solution.py:99
  225.4 25.8 %reduce-scatter.27.cloned.1.call-done = f32[256,8]{1,0:T(8,128)} async-done(((f32[2048,8]{1,0:T(8,128)}), f32[256,8]{1,0:T(8,128)}) %reduce-scatter.27.cloned.1.call-update) | async-done | bytes 8208
  254.3 9.9 %fusion.50 = f32[2,4,256]{2,0,1:T(2,128)S(1)} fusion(f32[2,4,256]{2,0,1:T(2,128)S(1)} %fusion.62, f32[2,4,256]{2,0,1:T(2,128)S(1)} %copy.140, f32[2,5,2048]{2,0,1:T(2,128)S(1)} %all_gather.25, f32[4,256,2048]{2,1,0:T(8,128)} %param.13, f32[4,256]{1,0:T(4,128)S(1)} %get-tuple-element.121, f32[]{:T(128)} %bitcast, f32[4,256]{1,0:T(4,128)S(1)} %compare_convert_fusion, ...), kind=kOutput, calls=%fused_computation.75 | convolution fusion | flops 50345984 | bytes 8511492 | tf_op jit(solution)/shard_map/lij,plj->pli/dot_general | solution.py:99
  289.0 9.4 %all_gather.26 = f32[2,5,2048]{2,0,1:T(2,128)S(1)} all-gather(f32[2,5,256]{2,0,1:T(2,128)S(1)} %pad_maximum_fusion.25), channel_id=1, replica_groups=mesh['inner'=4,'outer'=8] {'outer'}, dimensions={2}, use_global_device_ids=true | all-gather | bytes 92160 | tf_op jit(solution)/shard_map/all_gather | solution.py:97
  318.5 14.3 %all-reduce.2 = (f32[2,4,40]{2,0,1:T(2,128)S(1)}, f32[2,4,40]{2,0,1:T(2,128)}) all-reduce(f32[2,4,40]{2,0,1:T(2,128)S(1)} %copy.83, f32[2,4,40]{2,0,1:T(2,128)S(1)} %copy.87), channel_id=1, replica_groups=mesh['inner'=4,'outer'=8] {'outer'}, use_global_device_ids=true, to_apply=%region_5.6 | all-reduce | flops 640 | bytes 5120 | tf_op jit(solution)/shard_map/psum | solution.py:34
  333.0 10.4 %reduce-scatter.29.cloned.1.call-done = f32[256,8]{1,0:T(8,128)} async-done(((f32[2048,8]{1,0:T(8,128)}), f32[256,8]{1,0:T(8,128)}) %reduce-scatter.29.cloned.1.call-update) | async-done | bytes 8208
  346.7 10.4 %fusion.45 = f32[2,4,256]{2,0,1:T(2,128)S(1)} fusion(f32[2,4,256]{2,0,1:T(2,128)S(1)} %fusion.61, f32[2,4,256]{2,0,1:T(2,128)S(1)} %copy.142, f32[2,5,2048]{2,0,1:T(2,128)S(1)} %all_gather.26, f32[4,256,2048]{2,1,0:T(8,128)} %param.13, f32[4,256]{1,0:T(4,128)S(1)} %get-tuple-element.122, f32[]{:T(128)} %bitcast, f32[4,256]{1,0:T(4,128)S(1)} %compare_convert_fusion, ...), kind=kOutput, calls=%fused_computation.69 | convolution fusion | flops 50345984 | bytes 8511492 | tf_op jit(solution)/shard_map/lij,plj->pli/dot_general | solution.py:99
  388.5 26.8 %reduce-scatter.31.cloned.1.call-done = f32[256,8]{1,0:T(8,128)} async-done(((f32[2048,8]{1,0:T(8,128)}), f32[256,8]{1,0:T(8,128)}) %reduce-scatter.31.cloned.1.call-update) | async-done | bytes 8208
  418.4 9.9 %fusion.40 = f32[2,4,256]{2,0,1:T(2,128)S(1)} fusion(f32[2,4,256]{2,0,1:T(2,128)} %fusion.60, f32[2,4,256]{2,0,1:T(2,128)S(1)} %copy.144, f32[2,5,2048]{2,0,1:T(2,128)S(1)} %all_gather.27, f32[4,256,2048]{2,1,0:T(8,128)} %param.13, f32[4,256]{1,0:T(4,128)S(1)} %get-tuple-element.120, f32[]{:T(128)} %bitcast, f32[4,256]{1,0:T(4,128)S(1)} %compare_convert_fusion, ...), kind=kOutput, calls=%fused_computation.63 | convolution fusion | flops 50345984 | bytes 8511492 | tf_op jit(solution)/shard_map/lij,plj->pli/dot_general | solution.py:99
  503.2 12.7 %reduce-scatter.33.cloned.1.call-done = f32[256,8]{1,0:T(8,128)} async-done(((f32[2048,8]{1,0:T(8,128)}), f32[256,8]{1,0:T(8,128)}) %reduce-scatter.33.cloned.1.call-update) | async-done | bytes 8208
  529.3 13.2 %all-reduce.1 = (f32[2,4,40]{2,0,1:T(2,128)}, f32[2,4,40]{2,0,1:T(2,128)}) all-reduce(f32[2,4,40]{2,0,1:T(2,128)} %copy.91, f32[2,4,40]{2,0,1:T(2,128)} %copy.99), channel_id=1, replica_groups=mesh['inner'=4,'outer'=8] {'outer'}, use_global_device_ids=true, to_apply=%region_9.10 | all-reduce | flops 640 | bytes 5120 | tf_op jit(solution)/shard_map/psum | solution.py:34
  543.6 10.1 %fusion.35 = f32[2,4,256]{2,0,1:T(2,128)S(1)} fusion(f32[2,4,256]{2,0,1:T(2,128)S(1)} %fusion.59, f32[2,4,256]{2,0,1:T(2,128)} %copy.146, f32[2,5,2048]{2,0,1:T(2,128)S(1)} %all_gather.28, f32[4,256,2048]{2,1,0:T(8,128)} %param.13, f32[2,4,256]{2,0,1:T(2,128)S(1)} %fusion.196, f32[]{:T(128)} %bitcast.65, f32[4,256]{1,0:T(4,128)S(1)} %copy-done.71, ...), kind=kOutput, calls=%fused_computation.57 | convolution fusion | flops 50343936 | bytes 8511492 | tf_op jit(solution)/shard_map/lij,plj->pli/dot_general | solution.py:99
  587.8 25.2 %reduce-scatter.35.cloned.1.call-done = f32[256,8]{1,0:T(8,128)} async-done(((f32[2048,8]{1,0:T(8,128)}), f32[256,8]{1,0:T(8,128)}) %reduce-scatter.35.cloned.1.call-update) | async-done | bytes 8208
  616.8 9.9 %fusion.30 = f32[2,4,256]{2,0,1:T(2,128)S(1)} fusion(f32[2,4,256]{2,0,1:T(2,128)} %fusion.58, f32[2,4,256]{2,0,1:T(2,128)} %copy.148, f32[2,5,2048]{2,0,1:T(2,128)S(1)} %all_gather.29, f32[4,256,2048]{2,1,0:T(8,128)} %param.13, f32[]{:T(128)} %bitcast.65, f32[4,256]{1,0:T(4,128)S(1)} %get-tuple-element.121, f32[4,256]{1,0:T(4,128)S(1)} %compare_convert_fusion, ...), kind=kOutput, calls=%fused_computation.51 | convolution fusion | flops 50345984 | bytes 8511492 | tf_op jit(solution)/shard_map/lij,plj->pli/dot_general | solution.py:99
  658.9 9.4 %all_gather.30 = f32[2,5,2048]{2,0,1:T(2,128)S(1)} all-gather(f32[2,5,256]{2,0,1:T(2,128)S(1)} %pad_maximum_fusion.29), channel_id=1, replica_groups=mesh['inner'=4,'outer'=8] {'outer'}, dimensions={2}, use_global_device_ids=true | all-gather | bytes 92160 | tf_op jit(solution)/shard_map/all_gather | solution.py:97
  699.6 14.9 %reduce-scatter.37.cloned.1.call-done = f32[256,8]{1,0:T(8,128)} async-done(((f32[2048,8]{1,0:T(8,128)}), f32[256,8]{1,0:T(8,128)}) %reduce-scatter.37.cloned.1.call-update) | async-done | bytes 8208
  729.1 13.5 %all-reduce = (f32[2,4,40]{2,0,1:T(2,128)}, f32[2,4,40]{2,0,1:T(2,128)}) all-reduce(f32[2,4,40]{2,0,1:T(2,128)} %copy.107, f32[2,4,40]{2,0,1:T(2,128)} %copy.103), channel_id=1, replica_groups=mesh['inner'=4,'outer'=8] {'outer'}, use_global_device_ids=true, to_apply=%region_15.16 | all-reduce | flops 640 | bytes 5120 | tf_op jit(solution)/shard_map/psum | solution.py:34
  743.6 10.1 %fusion.25 = f32[2,4,256]{2,0,1:T(2,128)S(1)} fusion(f32[2,4,256]{2,0,1:T(2,128)S(1)} %fusion.57, f32[2,4,256]{2,0,1:T(2,128)} %copy.150, f32[2,5,2048]{2,0,1:T(2,128)S(1)} %all_gather.30, f32[4,256,2048]{2,1,0:T(8,128)} %param.13, f32[]{:T(128)} %bitcast.65, f32[4,256]{1,0:T(4,128)S(1)} %get-tuple-element.122, f32[4,256]{1,0:T(4,128)S(1)} %compare_convert_fusion, ...), kind=kOutput, calls=%fused_computation.45 | convolution fusion | flops 50345984 | bytes 8511492 | tf_op jit(solution)/shard_map/lij,plj->pli/dot_general | solution.py:99
  789.5 9.7 %all_gather.31 = f32[2,5,2048]{2,0,1:T(2,128)S(1)} all-gather(f32[2,5,256]{2,0,1:T(2,128)S(1)} %pad_maximum_fusion.30), channel_id=1, replica_groups=mesh['inner'=4,'outer'=8] {'outer'}, dimensions={2}, use_global_device_ids=true | all-gather | bytes 92160 | tf_op jit(solution)/shard_map/all_gather | solution.py:97
  799.2 23.2 %reduce-scatter.39.cloned.1.call-done = f32[256,8]{1,0:T(8,128)} async-done(((f32[2048,8]{1,0:T(8,128)}), f32[256,8]{1,0:T(8,128)}) %reduce-scatter.39.cloned.1.call-update) | async-done | bytes 8208
  823.9 10.4 %fusion.20 = f32[2,4,256]{2,0,1:T(2,128)S(1)} fusion(f32[2,4,256]{2,0,1:T(2,128)S(1)} %copy-done.76, f32[2,4,256]{2,0,1:T(2,128)S(1)} %copy.152, f32[2,5,2048]{2,0,1:T(2,128)S(1)} %all_gather.31, f32[4,256,2048]{2,1,0:T(8,128)} %param.13, f32[]{:T(128)} %bitcast.65, f32[4,256]{1,0:T(4,128)S(1)} %get-tuple-element.120, ...), kind=kOutput, calls=%fused_computation.39 | convolution fusion | flops 50345984 | bytes 8511492 | tf_op jit(solution)/shard_map/lij,plj->pli/dot_general | solution.py:99
  (614 shorter events, 488.6 us)
Async XLA Ops:
  7.2 160.2 %reduce-scatter.25.cloned.1.call-start = ((), (), s32[]{:S(2)}) async-start(), calls=%async_computation.8 | async-start | bytes 1179648
  11.0 50.2 %collective-permute-start.12 = (f32[40,40]{0,1:T(8,128)S(1)}, f32[40,40]{0,1:T(8,128)S(1)}, u32[]{:S(2)}, u32[]{:S(2)}) collective-permute-start(f32[40,40]{0,1:T(8,128)S(1)} %slice_bitcast_fusion.17), channel_id=1, source_target_pairs={{0,8},{8,16},{16,24},{1,9},{9,17},{17,25},{2,10},{10,18},{18,26},{... | collective-permute-start | bytes 19208 | tf_op jit(solution)/shard_map/ppermute | solution.py:29
  16.2 49.0 %collective-permute-start.11 = (f32[2,40,512]{2,1,0:T(8,128)S(1)}, f32[2,40,512]{2,1,0:T(8,128)}, u32[]{:S(2)}, u32[]{:S(2)}) collective-permute-start(f32[2,40,512]{2,1,0:T(8,128)S(1)} %get-tuple-element.87), channel_id=1, source_target_pairs={{0,8},{8,16},{16,24},{1,9},{9,17},{17,25},{2,10},{10,18},{18,26},{... | collective-permute-start | bytes 491528 | tf_op jit(solution)/shard_map/ppermute | solution.py:29
  19.7 50.2 %collective-permute-start.10 = (f32[2,40,512]{2,1,0:T(8,128)}, f32[2,40,512]{2,1,0:T(8,128)S(1)}, u32[]{:S(2)}, u32[]{:S(2)}) collective-permute-start(f32[2,40,512]{2,1,0:T(8,128)} %get-tuple-element.86), channel_id=1, source_target_pairs={{8,0},{16,8},{24,16},{9,1},{17,9},{25,17},{10,2},{18,10},{26,18},{... | collective-permute-start | bytes 491528 | tf_op jit(solution)/shard_map/ppermute | solution.py:29
  65.2 50.2 %collective-permute-start.2 = (f32[256,2048]{1,0:T(8,128)}, f32[256,2048]{1,0:T(8,128)S(1)}, u32[]{:S(2)}, u32[]{:S(2)}) collective-permute-start(f32[256,2048]{1,0:T(8,128)} %slice_bitcast_fusion), channel_id=1, source_target_pairs={{0,8},{8,16},{16,24},{1,9},{9,17},{17,25},{2,10},{10,18},{18,26},{... | collective-permute-start | bytes 6291464 | tf_op jit(solution)/shard_map/ppermute | solution.py:29
  79.0 53.9 %collective-permute-start.21 = (f32[2,40,512]{2,1,0:T(8,128)}, f32[2,40,512]{2,1,0:T(8,128)}, u32[]{:S(2)}, u32[]{:S(2)}) collective-permute-start(f32[2,40,512]{2,1,0:T(8,128)} %get-tuple-element.81), channel_id=1, source_target_pairs={{0,8},{8,16},{16,24},{1,9},{9,17},{17,25},{2,10},{10,18},{18,26},{... | collective-permute-start | bytes 491528 | tf_op jit(solution)/shard_map/ppermute | solution.py:29
  95.6 89.2 %collective-permute-start.20 = (f32[2,40,512]{2,1,0:T(8,128)}, f32[2,40,512]{2,1,0:T(8,128)}, u32[]{:S(2)}, u32[]{:S(2)}) collective-permute-start(f32[2,40,512]{2,1,0:T(8,128)} %get-tuple-element.80), channel_id=1, source_target_pairs={{8,0},{16,8},{24,16},{9,1},{17,9},{25,17},{10,2},{18,10},{26,18},{... | collective-permute-start | bytes 491528 | tf_op jit(solution)/shard_map/ppermute | solution.py:29
  100.1 114.3 %collective-permute-start.15 = (f32[2,160,1]{2,1,0:T(8,128)}, f32[2,160,1]{2,1,0:T(8,128)}, u32[]{:S(2)}, u32[]{:S(2)}) collective-permute-start(f32[2,160,1]{2,1,0:T(8,128)} %get-tuple-element.73), channel_id=1, source_target_pairs={{0,1},{1,2},{2,3},{3,4},{4,5},{5,6},{6,7},{8,9},{9,10},{10,11},{11... | collective-permute-start | bytes 3848 | tf_op jit(solution)/shard_map/ppermute | solution.py:45
  102.1 112.3 %collective-permute-start.19 = (f32[2,160,1]{2,1,0:T(8,128)}, f32[2,160,1]{2,1,0:T(8,128)}, u32[]{:S(2)}, u32[]{:S(2)}) collective-permute-start(f32[2,160,1]{2,1,0:T(8,128)} %get-tuple-element.74), channel_id=1, source_target_pairs={{1,0},{2,1},{3,2},{4,3},{5,4},{6,5},{7,6},{9,8},{10,9},{11,10},{12... | collective-permute-start | bytes 3848 | tf_op jit(solution)/shard_map/ppermute | solution.py:47
  132.3 118.8 %reduce-scatter.27.cloned.1.call-start = ((), (), s32[]{:S(2)}) async-start(), calls=%async_computation.9 | async-start | bytes 1179648
  214.1 129.4 %reduce-scatter.29.cloned.1.call-start = ((), (), s32[]{:S(2)}) async-start(), calls=%async_computation.10 | async-start | bytes 1179648
  218.0 89.6 %collective-permute-start.30 = (f32[2,40,512]{2,1,0:T(8,128)}, f32[2,40,512]{2,1,0:T(8,128)}, u32[]{:S(2)}, u32[]{:S(2)}) collective-permute-start(f32[2,40,512]{2,1,0:T(8,128)} %get-tuple-element.69), channel_id=1, source_target_pairs={{0,8},{8,16},{16,24},{1,9},{9,17},{17,25},{2,10},{10,18},{18,26},{... | collective-permute-start | bytes 491528 | tf_op jit(solution)/shard_map/ppermute | solution.py:29
  221.3 88.0 %collective-permute-start.29 = (f32[2,40,512]{2,1,0:T(8,128)}, f32[2,40,512]{2,1,0:T(8,128)}, u32[]{:S(2)}, u32[]{:S(2)}) collective-permute-start(f32[2,40,512]{2,1,0:T(8,128)} %get-tuple-element.68), channel_id=1, source_target_pairs={{8,0},{16,8},{24,16},{9,1},{17,9},{25,17},{10,2},{18,10},{26,18},{... | collective-permute-start | bytes 491528 | tf_op jit(solution)/shard_map/ppermute | solution.py:29
  307.2 108.0 %reduce-scatter.31.cloned.1.call-start = ((), (), s32[]{:S(2)}) async-start(), calls=%async_computation.11 | async-start | bytes 1179648
  377.7 138.3 %reduce-scatter.33.cloned.1.call-start = ((), (), s32[]{:S(2)}) async-start(), calls=%async_computation.12 | async-start | bytes 1179648
  387.9 51.5 %collective-permute-start.36 = (f32[2,4,40]{2,0,1:T(2,128)}, f32[2,4,40]{2,0,1:T(2,128)}, u32[]{:S(2)}, u32[]{:S(2)}) collective-permute-start(f32[2,4,40]{2,0,1:T(2,128)} %add.355), channel_id=1, source_target_pairs={{0,4},{1,5},{2,6},{3,7},{4,0},{5,1},{6,2},{7,3},{8,12},{9,13},{10,... | collective-permute-start | bytes 3848 | tf_op jit(solution)/shard_map/ppermute | solution.py:20
  478.9 134.1 %reduce-scatter.35.cloned.1.call-start = ((), (), s32[]{:S(2)}) async-start(), calls=%async_computation.13 | async-start | bytes 1179648
  575.8 138.7 %reduce-scatter.37.cloned.1.call-start = ((), (), s32[]{:S(2)}) async-start(), calls=%async_computation.14 | async-start | bytes 1179648
  587.2 50.5 %collective-permute-start.54 = (f32[2,4,40]{2,0,1:T(2,128)}, f32[2,4,40]{2,0,1:T(2,128)}, u32[]{:S(2)}, u32[]{:S(2)}) collective-permute-start(f32[2,4,40]{2,0,1:T(2,128)} %add.376), channel_id=1, source_target_pairs={{0,4},{1,5},{2,6},{3,7},{4,0},{5,1},{6,2},{7,3},{8,12},{9,13},{10,... | collective-permute-start | bytes 3848 | tf_op jit(solution)/shard_map/ppermute | solution.py:20
  677.1 145.4 %reduce-scatter.39.cloned.1.call-start = ((), (), s32[]{:S(2)}) async-start(), calls=%async_computation.15 | async-start | bytes 1179648
  754.6 80.5 %collective-permute-start.73 = (f32[2,40,512]{2,1,0:T(8,128)}, f32[2,40,512]{2,1,0:T(8,128)}, u32[]{:S(2)}, u32[]{:S(2)}) collective-permute-start(f32[2,40,512]{2,1,0:T(8,128)} %get-tuple-element.21), channel_id=1, source_target_pairs={{0,8},{8,16},{16,24},{1,9},{9,17},{17,25},{2,10},{10,18},{18,26},{... | collective-permute-start | bytes 491528 | tf_op jit(solution)/shard_map/ppermute | solution.py:29
  758.0 78.7 %collective-permute-start.72 = (f32[2,40,512]{2,1,0:T(8,128)}, f32[2,40,512]{2,1,0:T(8,128)}, u32[]{:S(2)}, u32[]{:S(2)}) collective-permute-start(f32[2,40,512]{2,1,0:T(8,128)} %get-tuple-element.20), channel_id=1, source_target_pairs={{8,0},{16,8},{24,16},{9,1},{17,9},{25,17},{10,2},{18,10},{26,18},{... | collective-permute-start | bytes 491528 | tf_op jit(solution)/shard_map/ppermute | solution.py:29
  761.1 78.0 %collective-permute-start.67 = (f32[2,160,1]{2,1,0:T(8,128)}, f32[2,160,1]{2,1,0:T(8,128)}, u32[]{:S(2)}, u32[]{:S(2)}) collective-permute-start(f32[2,160,1]{2,1,0:T(8,128)} %get-tuple-element.22), channel_id=1, source_target_pairs={{0,1},{1,2},{2,3},{3,4},{4,5},{5,6},{6,7},{8,9},{9,10},{10,11},{11... | collective-permute-start | bytes 3848 | tf_op jit(solution)/shard_map/ppermute | solution.py:45
  766.6 72.5 %collective-permute-start.71 = (f32[2,160,1]{2,1,0:T(8,128)}, f32[2,160,1]{2,1,0:T(8,128)}, u32[]{:S(2)}, u32[]{:S(2)}) collective-permute-start(f32[2,160,1]{2,1,0:T(8,128)} %get-tuple-element.24), channel_id=1, source_target_pairs={{1,0},{2,1},{3,2},{4,3},{5,4},{6,5},{7,6},{9,8},{10,9},{11,10},{12... | collective-permute-start | bytes 3848 | tf_op jit(solution)/shard_map/ppermute | solution.py:47
  (157 other events, 3568.1 us)
Sparse Core Ops, SparseCore 0:
  132.5 34.8 reduce-scatter.24
  214.2 36.9 reduce-scatter.26
  307.3 36.0 reduce-scatter.28
  377.8 37.3 reduce-scatter.30
  479.0 36.8 reduce-scatter.32
  575.9 37.0 reduce-scatter.34
  677.2 37.2 reduce-scatter.36
  785.9 36.4 reduce-scatter.38
